TPU v7x, 8 devices: a whole 2x2x1 slice. The times are simulated.
8 devices in a mesh: fsdp: 8 (over z, y, x, core).
Axes of the slice: x: 2, y: 2, z: 1, core: 2. Of those that a mesh axis runs over, the one named last changes fastest.
Arguments:
- x: bfloat16 [64, 384, 512], P('fsdp')
- lengths: int32 [64], P('fsdp')
- d_y: bfloat16 [64, 384, 512], P('fsdp')
- w_attn: bfloat16 [2, 4, 512, 512], P(None, None, 'fsdp')
- b_attn: bfloat16 [2, 4, 512], P(None, None, 'fsdp')
- ln_par: bfloat16 [2, 4, 512], P(None, None, 'fsdp')
- w_up: bfloat16 [2, 512, 2048], P(None, 'fsdp')
- b_up: bfloat16 [2, 2048], P(None, 'fsdp')
- w_down: bfloat16 [2, 2048, 512], P(None, 'fsdp')
- b_down: bfloat16 [2, 512], P(None, 'fsdp')
Outputs:
- output 1: bfloat16 [64, 384, 512], P('fsdp')
- output 2: float32 [2, 4, 512, 512], P(None, None, 'fsdp')
- output 3: float32 [2, 4, 512], P(None, None, 'fsdp')
- output 4: float32 [2, 4, 512], P(None, None, 'fsdp')
- output 5: float32 [2, 512, 2048], P(None, 'fsdp')
- output 6: float32 [2, 2048], P(None, 'fsdp')
- output 7: float32 [2, 2048, 512], P(None, 'fsdp')
- output 8: float32 [2, 512], P(None, 'fsdp')
All inputs are finite; a program needn't handle non-finite values.
Results may differ from a plain program's by a relative error of at most 0.0135649.
Values are sent between devices in bfloat16 or wider.
A program may use at most 1 GiB of HBM per device.

v0:
```python
import math
import jax
import jax.numpy as jnp
from jax import lax
from jax.experimental import pallas as pl
from jax.experimental.pallas import tpu as pltpu
from jax.sharding import PartitionSpec as P

HEAD_DIM = 64
EPS = 1e-5
THETA = 10000.0
NEG_BIG = -1e30
BF16 = jnp.bfloat16
F32 = jnp.float32
VMEM_BYTES = 60 * 1024 * 1024
GROUP = 256
HEADS_GROUP = 4
KEY_BLOCK = 128
FWD_ROWS = 384
BWD_ROWS = 512

NN, NT, TN = (1, 0), (1, 1), (0, 0)


def mm(a, b, dims=NN):
    return lax.dot_general(a, b, (((dims[0],), (dims[1],)), ((), ())), preferred_element_type=F32)


def line(ref, i):
    return ref[i:i + 1, :]


def add_line(ref, i, block):
    ref[i:i + 1, :] += jnp.sum(block, axis=0, keepdims=True)


def row_mean(block):
    return jnp.mean(block, axis=-1, keepdims=True)


def row_sum(block):
    return jnp.sum(block, axis=-1, keepdims=True)


def square(w_ref, i):
    model = w_ref.shape[-1]
    return w_ref[:, i * HEAD_DIM:(i + 1) * HEAD_DIM, :].reshape(model, model)


def rotary_tables(seq_len):
    half_dim = HEAD_DIM // 2
    freq_pos = (jnp.arange(2 * HEAD_DIM) % half_dim).astype(F32)
    inv_freq = 1.0 / (THETA ** (freq_pos * (2.0 / HEAD_DIM)))
    angles = jnp.arange(seq_len, dtype=F32)[:, None] * inv_freq[None, :]
    return jnp.cos(angles), jnp.sin(angles)


def normalize(x_f32):
    centered = x_f32 - row_mean(x_f32)
    rstd = lax.rsqrt(row_mean(centered * centered) + EPS)
    return centered * rstd, rstd


def norm_bwd(d_h, x_hat, rstd, gain):
    d_hat = d_h * gain
    mean_d = row_mean(d_hat)
    mean_dx = row_mean(d_hat * x_hat)
    return rstd * (d_hat - mean_d - x_hat * mean_dx)


def halves(block, lo):
    mid = lo + GROUP // 2
    return block[:, lo:mid], block[:, mid:lo + GROUP]


def rot_halves(first, second, cos_tab, sin_tab):
    return first * cos_tab - second * sin_tab, second * cos_tab + first * sin_tab


def unrot_halves(first, second, cos_tab, sin_tab):
    return first * cos_tab + second * sin_tab, second * cos_tab - first * sin_tab


def head_masks():
    lane = lax.broadcasted_iota(jnp.int32, (1, GROUP), 1)
    qk = [((lane % 128) // 32 == h).astype(F32).astype(BF16) for h in range(HEADS_GROUP)]
    vo = [(lane // 64 == h).astype(F32).astype(BF16) for h in range(HEADS_GROUP)]
    return qk, vo


def stack_masked(block, masks):
    return jnp.concatenate([block * m for m in masks], axis=0)


def for_key_width(length, seq_len, body):
    blocks = (length + KEY_BLOCK - 1) // KEY_BLOCK
    for n in range(1, seq_len // KEY_BLOCK + 1):
        @pl.when(blocks == n)
        def _(n=n):
            body(n * KEY_BLOCK)


def attn_fwd_kernel(len_ref, x_ref, w_ref, vec_ref, cos_ref, sin_ref, q_ref, k_ref, v_ref, p_ref, ctx_ref, mid_ref):
    seq_len, model = x_ref.shape[1:]
    length = len_ref[pl.program_id(0)]
    x_hat, _ = normalize(x_ref[0].astype(F32))
    h_one = (x_hat * line(vec_ref, 4) + line(vec_ref, 5)).astype(BF16)
    cos_tab, sin_tab = cos_ref[:], sin_ref[:]
    for i, out in enumerate((q_ref, k_ref)):
        proj = mm(h_one, square(w_ref, i)) + line(vec_ref, i)
        if i == 0:
            proj = proj * (HEAD_DIM ** -0.5)
        for g in range(model // GROUP):
            lo = g * GROUP
            first, second = rot_halves(*halves(proj, lo), cos_tab, sin_tab)
            out[0, :, lo:lo + GROUP] = jnp.concatenate([first.astype(BF16), second.astype(BF16)], axis=1)
    proj = mm(h_one, square(w_ref, 2)) + line(vec_ref, 2)
    v_ref[0] = proj.astype(BF16)
    qk_masks, vo_masks = head_masks()

    def attend(width):
        valid = lax.broadcasted_iota(jnp.int32, (1, width), 1) < length
        for g in range(model // GROUP):
            lo = g * GROUP
            k_cat = stack_masked(k_ref[0, 0:width, lo:lo + GROUP], qk_masks)
            scores = mm(q_ref[0, :, lo:lo + GROUP], k_cat, NT)
            probs = []
            for h in range(HEADS_GROUP):
                s_h = jnp.where(valid, scores[:, h * width:(h + 1) * width], NEG_BIG)
                e_h = jnp.exp(s_h - jnp.max(s_h, axis=-1, keepdims=True))
                p_h = (e_h * (1.0 / row_sum(e_h))).astype(BF16)
                base = (g * HEADS_GROUP + h) * seq_len
                p_ref[0, :, base:base + width] = p_h
                probs.append(p_h)
            v_cat = stack_masked(v_ref[0, 0:width, lo:lo + GROUP], vo_masks)
            ctx_ref[0, :, lo:lo + GROUP] = mm(jnp.concatenate(probs, axis=1), v_cat).astype(BF16)

    for_key_width(length, seq_len, attend)
    attn_out = mm(ctx_ref[0], square(w_ref, 3))
    mid_ref[0] = (x_ref[0].astype(F32) + attn_out + line(vec_ref, 3)).astype(BF16)


def mlp_fwd_kernel(mid_ref, w_ref, vec_ref, y_ref, act_ref, slope_ref):
    model = mid_ref.shape[1]
    mid = mid_ref[:].astype(F32)
    x_hat, _ = normalize(mid)
    h_two = (x_hat * line(vec_ref, 6) + line(vec_ref, 7)).astype(BF16)
    for c in range(4):
        cols = slice(c * model, (c + 1) * model)
        pre = mm(h_two, square(w_ref, c)) + line(vec_ref, 9 + c)
        cdf = 0.5 * lax.erf(pre * (1.0 / math.sqrt(2.0))) + 0.5
        density = jnp.exp(pre * pre * -0.5) * (1.0 / math.sqrt(2.0 * math.pi))
        act_ref[:, cols] = (pre * cdf).astype(BF16)
        slope_ref[:, cols] = cdf + pre * density
    out = mm(act_ref[:], w_ref[:, 256:512, :].reshape(4 * model, model))
    y_ref[:] = (mid + out + line(vec_ref, 8)).astype(BF16)


def mlp_bwd_scatter_kernel(dout_ref, mid_ref, act_ref, slope_ref, w_ref, vec_ref, ga_ref, dmid_ref, gw_ref, gs_ref, out_ref,
                           dpre_ref, own_ref, *rest):
    job = Scatter(ga_ref, own_ref, out_ref, rest[:6], rest[6:])
    step, last = pl.program_id(0), pl.num_programs(0) - 1
    pl.when(step == 0)(job.stage_one)
    pl.when(step == 1)(job.stage_two)
    pl.when(step == last - 1)(job.stage_three)
    mlp_bwd_kernel(dout_ref, mid_ref, act_ref, slope_ref, w_ref, vec_ref, dmid_ref, gw_ref, gs_ref, dpre_ref)
    pl.when(step == last)(job.stage_four)


def mlp_bwd_kernel(dout_ref, mid_ref, act_ref, slope_ref, w_ref, vec_ref, dmid_ref, gw_ref, gs_ref, dpre_ref):
    model = mid_ref.shape[1]

    @pl.when(pl.program_id(0) == 0)
    def _():
        gw_ref[:] = jnp.zeros_like(gw_ref)
        gs_ref[:] = jnp.zeros_like(gs_ref)

    x_hat, rstd = normalize(mid_ref[:].astype(F32))
    h_two = (x_hat * line(vec_ref, 6) + line(vec_ref, 7)).astype(BF16)
    d_out = dout_ref[:]
    d_h = None
    for c in range(4):
        cols = slice(c * model, (c + 1) * model)
        d_act = mm(d_out, w_ref[2 * c:2 * c + 2, 256:512, :].reshape(model, model), NT)
        d_pre = d_act * slope_ref[:, cols]
        add_line(gs_ref, c, d_pre)
        dpre_ref[:, cols] = d_pre.astype(BF16)
    for c in range(4):
        cols = slice(c * model, (c + 1) * model)
        gw_ref[2 * c:2 * c + 2, 256:512, :] += mm(act_ref[:, cols], d_out, TN).reshape(2, 256, model)
        gw_ref[:, c * 64:(c + 1) * 64, :] += mm(h_two, dpre_ref[:, cols], TN).reshape(8, 64, model)
        part = mm(dpre_ref[:, cols], square(w_ref, c), NT)
        d_h = part if d_h is None else d_h + part
    d_out_f32 = d_out.astype(F32)
    add_line(gs_ref, 4, d_out_f32)
    add_line(gs_ref, 5, d_h * x_hat)
    add_line(gs_ref, 6, d_h)
    dmid_ref[:] = (d_out_f32 + norm_bwd(d_h, x_hat, rstd, line(vec_ref, 6))).astype(BF16)


def attn_bwd_kernel(len_ref, dmid_ref, x_ref, q_ref, k_ref, v_ref, p_ref, ctx_ref, w_ref, vec_ref, cos_ref, sin_ref,
                    dx_ref, gw_ref, gs_ref, dctx_ref, dq_ref, dk_ref, dv_ref):
    seq_len, model = x_ref.shape[1:]
    length = len_ref[pl.program_id(0)]

    @pl.when(pl.program_id(0) == 0)
    def _():
        gw_ref[:] = jnp.zeros_like(gw_ref)
        gs_ref[:] = jnp.zeros_like(gs_ref)

    d_mid = dmid_ref[0]
    d_mid_f32 = d_mid.astype(F32)
    add_line(gs_ref, 3, d_mid_f32)
    gw_ref[:, 192:256, :] += mm(ctx_ref[0], d_mid, TN).reshape(8, 64, model)
    dctx_ref[:] = mm(d_mid, square(w_ref, 3), NT).astype(BF16)
    qk_masks, vo_masks = head_masks()

    def attend(width):
        for g in range(model // GROUP):
            lo = g * GROUP
            d_ctx = dctx_ref[:, lo:lo + GROUP]
            d_probs = mm(d_ctx, stack_masked(v_ref[0, 0:width, lo:lo + GROUP], vo_masks), NT)
            ds_list, dst_list, pt_list = [], [], []
            for h in range(HEADS_GROUP):
                base = (g * HEADS_GROUP + h) * seq_len
                p_bf = p_ref[0, :, base:base + width]
                p_h = p_bf.astype(F32)
                dp_h = d_probs[:, h * width:(h + 1) * width]
                ds_h = (p_h * (dp_h - row_sum(dp_h * p_h))).astype(BF16)
                ds_list.append(ds_h)
                dst_list.append(ds_h.T)
                pt_list.append(p_bf.T)
            k_cat = stack_masked(k_ref[0, 0:width, lo:lo + GROUP], qk_masks)
            dq_ref[:, lo:lo + GROUP] = mm(jnp.concatenate(ds_list, axis=1), k_cat)
            q_cat = stack_masked(q_ref[0, :, lo:lo + GROUP], qk_masks)
            dk_ref[0:width, lo:lo + GROUP] = mm(jnp.concatenate(dst_list, axis=1), q_cat)
            do_cat = stack_masked(d_ctx, vo_masks)
            dv_ref[0:width, lo:lo + GROUP] = mm(jnp.concatenate(pt_list, axis=1), do_cat)
        if width < seq_len:
            dk_ref[width:, :] = jnp.zeros((seq_len - width, model), F32)
            dv_ref[width:, :] = jnp.zeros((seq_len - width, model), F32)

    for_key_width(length, seq_len, attend)
    cos_tab, sin_tab = cos_ref[:], sin_ref[:]
    x_hat, rstd = normalize(x_ref[0].astype(F32))
    h_one = (x_hat * line(vec_ref, 4) + line(vec_ref, 5)).astype(BF16)
    d_h = None
    for i, src in enumerate((dq_ref, dk_ref, dv_ref)):
        if i < 2:
            pieces = []
            for g in range(model // GROUP):
                lo = g * GROUP
                pieces.extend(unrot_halves(*halves(src, lo), cos_tab, sin_tab))
            d_proj = jnp.concatenate(pieces, axis=1)
            if i == 0:
                d_proj = d_proj * (HEAD_DIM ** -0.5)
        else:
            d_proj = src[:]
        d_proj = d_proj.astype(BF16)
        add_line(gs_ref, i, d_proj.astype(F32))
        gw_ref[:, i * 64:(i + 1) * 64, :] += mm(h_one, d_proj, TN).reshape(8, 64, model)
        part = mm(d_proj, square(w_ref, i), NT)
        d_h = part if d_h is None else d_h + part
    add_line(gs_ref, 4, d_h * x_hat)
    add_line(gs_ref, 5, d_h)
    dx_ref[0] = (d_mid_f32 + norm_bwd(d_h, x_hat, rstd, line(vec_ref, 4))).astype(BF16)


def seq_spec(*tail):
    return pl.BlockSpec((1,) + tail, lambda b, *_: (b,) + (0,) * len(tail))


def row_spec(rows, cols):
    return pl.BlockSpec((rows, cols), lambda b, *_: (b, 0))


def whole(shape):
    return pl.BlockSpec(shape, lambda *_: (0,) * len(shape))


def params():
    return pltpu.CompilerParams(dimension_semantics=('arbitrary',), vmem_limit_bytes=VMEM_BYTES)


def cost(flops, nbytes):
    return pl.CostEstimate(flops=int(flops), bytes_accessed=int(nbytes), transcendentals=0)


def sds(shape, dtype):
    return jax.ShapeDtypeStruct(shape, dtype)


def attn_forward(lengths, x, w, vec, tables):
    n, seq_len, model = x.shape
    heads = model // HEAD_DIM
    act = sds(x.shape, BF16)
    spec = seq_spec(seq_len, model)
    return pl.pallas_call(
        attn_fwd_kernel,
        grid_spec=pltpu.PrefetchScalarGridSpec(
            num_scalar_prefetch=1, grid=(n,),
            in_specs=[spec, whole((8, 256, model)), whole(vec.shape), whole(tables[0].shape), whole(tables[1].shape)],
            out_specs=[spec, spec, spec, seq_spec(seq_len, heads * seq_len), spec, spec]),
        out_shape=[act, act, act, sds((n, seq_len, heads * seq_len), BF16), act, act],
        compiler_params=params(), cost_estimate=cost(16e9, 40e6), name='attn_fwd',
    )(lengths, x, w, vec, *tables)


def mlp_forward(mid, w, vec, rows):
    tokens, model = mid.shape
    return pl.pallas_call(
        mlp_fwd_kernel, grid=(tokens // rows,),
        in_specs=[row_spec(rows, model), whole(w.shape), whole(vec.shape)],
        out_specs=[row_spec(rows, model), row_spec(rows, 4 * model), row_spec(rows, 4 * model)],
        out_shape=[sds(mid.shape, BF16), sds((tokens, 4 * model), BF16), sds((tokens, 4 * model), F32)],
        compiler_params=params(), cost_estimate=cost(13e9, 50e6), name='mlp_fwd',
    )(mid, w, vec)


def mlp_backward(d_out, mid, act, slope, w, vec, rows, g_a=None):
    tokens, model = mid.shape
    wide = row_spec(rows, 4 * model)
    in_specs = [row_spec(rows, model), row_spec(rows, model), wide, wide, whole(w.shape), whole(vec.shape)]
    out_specs = [row_spec(rows, model), whole(w.shape), whole((8, model))]
    out_shape = [sds(mid.shape, BF16), sds(w.shape, F32), sds((8, model), F32)]
    scratch = [pltpu.VMEM((rows, 4 * model), BF16)]
    ins, kernel, extra = (d_out, mid, act, slope, w, vec), mlp_bwd_kernel, {}
    if g_a is not None:
        ins, kernel, extra = ins + (g_a,), mlp_bwd_scatter_kernel, {'collective_id': 2, 'has_side_effects': True}
        in_specs.append(pl.BlockSpec(memory_space=pl.ANY))
        out_specs.append(whole(g_a.shape[1:]))
        out_shape.append(sds(g_a.shape[1:], F32))
        n = g_a.shape[1] // PIECE
        scratch += [pltpu.VMEM((4,) + g_a.shape[1:], F32)] + scatter_bufs(n, PIECE, model) + scatter_sems(n)
    return pl.pallas_call(
        kernel, grid=(tokens // rows,), in_specs=in_specs, out_specs=out_specs, out_shape=out_shape, scratch_shapes=scratch,
        compiler_params=pltpu.CompilerParams(dimension_semantics=('arbitrary',), vmem_limit_bytes=VMEM_BYTES, **extra),
        cost_estimate=cost(26e9, 60e6), name='mlp_bwd',
    )(*ins)


def attn_backward(lengths, d_mid, x, saved, w, vec, tables):
    n, seq_len, model = x.shape
    heads = model // HEAD_DIM
    spec = seq_spec(seq_len, model)
    return pl.pallas_call(
        attn_bwd_kernel,
        grid_spec=pltpu.PrefetchScalarGridSpec(
            num_scalar_prefetch=1, grid=(n,),
            in_specs=[spec, spec, spec, spec, spec, seq_spec(seq_len, heads * seq_len), spec, whole((8, 256, model)),
                      whole(vec.shape), whole(tables[0].shape), whole(tables[1].shape)],
            out_specs=[spec, whole((8, 256, model)), whole((8, model))],
            scratch_shapes=[pltpu.VMEM((seq_len, model), BF16)] + [pltpu.VMEM((seq_len, model), F32)] * 3),
        out_shape=[sds(x.shape, BF16), sds((8, 256, model), F32), sds((8, model), F32)],
        compiler_params=params(), cost_estimate=cost(30e9, 50e6), name='attn_bwd',
    )(lengths, d_mid, x, *saved, w, vec, *tables)


MESH_ID = pl.DeviceIdType.MESH
PIECE = 64
SMALL = 32


def place():
    me = lax.axis_index('fsdp')
    core, x_bit, y_bit = lax.rem(me, 2), lax.rem(me // 2, 2), me // 4

    def rel(ry, rx, rc):
        return lax.rem(y_bit + ry, 2) * 4 + lax.rem(x_bit + rx, 2) * 2 + lax.rem(core + rc, 2)

    return rel


def peers(rel):
    return rel(0, 0, 1), rel(0, 1, 0), rel(1, 0, 0)


def greet(targets):
    barrier = pltpu.get_barrier_semaphore()
    for peer in targets:
        pl.semaphore_signal(barrier, device_id=(peer,), device_id_type=MESH_ID)
    pl.semaphore_wait(barrier, len(targets))


def remote(src, dst, sems, i, peer):
    return pltpu.make_async_remote_copy(src_ref=src, dst_ref=dst, send_sem=sems[0].at[i], recv_sem=sems[1].at[i],
                                        device_id=(peer,), device_id_type=MESH_ID)


def pack_small(dst, me, perm, b_attn, ln_par, b_up, b_down):
    part, model = b_attn.shape[-1], dst.shape[-1]
    spot = (lax.broadcasted_iota(jnp.int32, (part, model), 1) == lax.broadcasted_iota(jnp.int32, (part, model), 0) + me * part)
    spot = spot.astype(F32).astype(BF16)
    lane = lax.broadcasted_iota(jnp.int32, (4, model), 1)
    row = lax.broadcasted_iota(jnp.int32, (4, model), 0)
    here = (row == me // 2) & (lane // GROUP == lax.rem(me, 2))
    dst[:] = jnp.zeros_like(dst)
    for l in range(b_attn.shape[0]):
        base = l * SMALL // 2
        bias = mm(b_attn[l], spot)
        dst[base:base + 2, :] = permute_mm(bias[:2].astype(BF16), perm)
        dst[base + 2:base + 4, :] = bias[2:]
        dst[base + 4:base + 8, :] = mm(ln_par[l], spot)
        dst[base + 8:base + 9, :] = mm(b_down[l:l + 1, :], spot)
        up = b_up[l:l + 1, :].astype(F32)
        dst[base + 9:base + 13, :] = jnp.where(here, jnp.concatenate([up, up], axis=1), 0.0)


def permutation():
    old = lax.broadcasted_iota(jnp.int32, (GROUP, GROUP), 0)
    new = lax.broadcasted_iota(jnp.int32, (GROUP, GROUP), 1)
    half = HEAD_DIM // 2
    want = (new % 128) // half * HEAD_DIM + new // 128 * half + new % half
    return (old == want).astype(F32).astype(BF16)


def permute_mm(block, perm):
    return jnp.concatenate([mm(block[:, lo:lo + GROUP], perm) for lo in range(0, block.shape[1], GROUP)], axis=1)


def pack_attn(write, w_layer, perm):
    part = w_layer.shape[1]
    for i in range(4):
        rows = w_layer[i]
        write(slice(i * part, (i + 1) * part), permute_mm(rows, perm).astype(BF16) if i < 2 else rows)


def gather_kernel(w_attn, b_attn, ln_par, w_up, b_up, w_down, b_down, out_ref, vec0_ref, vec1_ref, attn_ref, mlp0_ref, mlp1_ref,
                  pack_ref, small_ref, send_sem, recv_sem):
    rel = place()
    core, px, py = peers(rel)
    me, diag = rel(0, 0, 0), rel(1, 1, 0)
    part, model = w_attn.shape[2:]
    perm = permutation()

    def put(rows, value):
        pack_ref[rows, :] = value

    def put_second(rows, value):
        attn_ref[rows, :] = value

    pack_small(small_ref, me, perm, b_attn, ln_par, b_up, b_down)
    pack_ref[4 * part:, :] = small_ref[:].astype(BF16)
    pack_attn(put, w_attn[0], perm)
    rows = pack_ref.shape[0]
    top, low = pl.ds(0, rows // 2), pl.ds(rows // 2, rows // 2)
    sems = (send_sem, recv_sem)
    greet((core, px, py))

    ids = iter(range(send_sem.shape[0]))

    def own(rows, peer):
        return remote(pack_ref.at[rows], out_ref.at[me, rows], sems, next(ids), peer)

    def pass_on(slot, rows, peer):
        return remote(out_ref.at[slot, rows], out_ref.at[slot, rows], sems, next(ids), peer)

    x_late, x_soon = own(top, px), own(low, px)
    y_soon, y_late = own(top, py), own(low, py)
    c_one, c_two = own(top, core), own(low, core)
    for copy in (x_soon, y_soon, x_late, y_late, c_one, c_two):
        copy.start()
    out_ref[pl.ds(me, 1)] = pack_ref[:][None]
    pack_attn(put_second, w_attn[1], perm)
    for l, mlp_ref in enumerate((mlp0_ref, mlp1_ref)):
        for c in range(4):
            mlp_ref[c * part:(c + 1) * part, :] = w_up[l, :, c * model:(c + 1) * model]
        mlp_ref[4 * part:, :] = w_down[l]
    on_x, on_y = pass_on(py, top, px), pass_on(px, low, py)
    steps = [(y_soon, on_x, pass_on(py, top, core)), (x_soon, on_y, pass_on(px, low, core)),
             (x_late, None, pass_on(px, top, core)), (y_late, None, pass_on(py, low, core)),
             (on_x, None, pass_on(diag, top, core)), (on_y, None, pass_on(diag, low, core))]
    for arrived, onward, across in steps:
        arrived.wait_recv()
        if onward:
            onward.start()
        across.start()
    from_core = [c_one, c_two] + [across for _, _, across in steps]
    for copy in from_core:
        copy.wait_recv()
    for copy in from_core + [arrived for arrived, _, _ in steps]:
        copy.wait_send()
    total = sum(out_ref[d, 4 * part:, :].astype(F32) for d in range(8))
    vec0_ref[:] = total[:SMALL // 2]
    vec1_ref[:] = total[SMALL // 2:]


def gather_head(*shards):
    part, model = shards[0].shape[2:]
    rows = 4 * part + SMALL
    vmem = pl.BlockSpec(memory_space=pltpu.VMEM)
    vec = sds((SMALL // 2, model), F32)
    mlp = sds((2 * GROUP, model), BF16)
    return pl.pallas_call(
        gather_kernel, in_specs=[vmem] * 7, out_specs=[vmem] * 6,
        out_shape=[sds((8, rows, model), BF16), vec, vec, sds((4 * part, model), BF16), mlp, mlp],
        scratch_shapes=[pltpu.VMEM((rows, model), BF16), pltpu.VMEM((SMALL, model), F32),
                        pltpu.SemaphoreType.DMA((14,)), pltpu.SemaphoreType.DMA((14,))],
        compiler_params=pltpu.CompilerParams(collective_id=0, has_side_effects=True, vmem_limit_bytes=VMEM_BYTES),
        cost_estimate=cost(1e9, 4e6), name='gather_head',
    )(*shards)


class Scatter:
    def __init__(self, src, own, out, bufs, sems, extra=()):
        rel = place()
        self.chunk = lambda r, c: rel(r // 2, r % 2, c)
        self.src, self.own, self.sems = src, own, sems
        self.targets = core, px, py = peers(rel)
        recv1, recv2, recv3, send2, send3, keep = bufs
        self.pieces = []
        for n, j in enumerate((0, 2, 1, 3)):
            self.pieces.append((src, own, out, j * PIECE, PIECE, j < 2, [b.at[n] for b in bufs]))
        for s, o, out_s, b in extra:
            self.pieces.append((s, o, out_s, 0, out_s.shape[0], True, b))
        self.first, self.second, self.third = [], [], []
        for n, (s, o, _, row, rows, x_first, b) in enumerate(self.pieces):
            self.first.append([remote(s.at[self.chunk(r, 1), pl.ds(row, rows)], b[0].at[r], sems[0:2], 4 * n + r, core)
                               for r in range(4)])
            self.second.append(remote(b[3], b[1], sems[2:4], n, px if x_first else py))
            self.third.append(remote(b[4], b[2], sems[4:6], n, py if x_first else px))
        self.local = [pltpu.make_async_copy(src.at[self.chunk(r, 0)], own.at[r], sems[6].at[r]) for r in range(4)]

    def stage_one(self):
        greet(self.targets)
        for copies in self.first:
            for copy in copies:
                copy.start()
        for copy in self.local:
            copy.start()

    def stage_two(self):
        for copy in self.local:
            copy.wait()
        for n, (_, o, _, row, rows, x_first, b) in enumerate(self.pieces):
            for copy in self.first[n]:
                copy.wait_recv()
            sent, kept = ((1, 3), (0, 2)) if x_first else ((2, 3), (0, 1))
            for i in range(2):
                b[3][i] = o[sent[i], row:row + rows, :] + b[0][sent[i]]
            for i in range(2):
                b[5][i] = o[kept[i], row:row + rows, :] + b[0][kept[i]]
            self.second[n].start()

    def stage_three(self):
        for n, (_, _, _, row, rows, _, b) in enumerate(self.pieces):
            self.second[n].wait_recv()
            b[4][:] = b[5][1] + b[1][1]
            b[5][0] = b[5][0] + b[1][0]
            self.third[n].start()

    def stage_four(self):
        for n, (_, _, out, row, rows, _, b) in enumerate(self.pieces):
            self.third[n].wait_recv()
            out[row:row + rows, :] = b[5][0] + b[2][:]
        for n, copies in enumerate(self.first):
            for copy in copies + [self.second[n], self.third[n]]:
                copy.wait_send()


def scatter_bufs(n, rows, model):
    lead = (n,) if n else ()
    shapes = [(4,), (2,), (), (2,), (), (2,)]
    return [pltpu.VMEM(lead + s + (rows, model), F32) for s in shapes]


def scatter_sems(n):
    dma = pltpu.SemaphoreType.DMA
    return [dma((4 * n,)), dma((4 * n,))] + [dma((n,))] * 4 + [dma((4,))]


def unpermute_lanes(x):
    half, wide = HEAD_DIM // 2, 2 * HEAD_DIM
    block = lax.broadcasted_iota(jnp.int32, (1, wide), 1) // half
    out = []
    for lo in range(0, x.shape[1], GROUP):
        pair = halves(x, lo)
        for j in range(2):
            acc = None
            for b in range(4):
                shift = half * (b - 2 * j - b // 2) % wide
                moved = pltpu.roll(pair[b % 2], shift, 1) if shift else pair[b % 2]
                acc = moved if acc is None else jnp.where(block == b, moved, acc)
            out.append(acc)
    return jnp.concatenate(out, axis=1)


def tail_kernel(ga_ref, sa1_ref, sa0_ref, sm1_ref, sm0_ref, out_ref, small_ref, own_ref, *rest):
    bufs, s_ref, so_ref, s_bufs, sems = rest[:6], rest[6], rest[7], rest[8:14], rest[14:]
    part = HEAD_DIM
    job = Scatter(ga_ref, own_ref, out_ref, bufs, sems, extra=[(s_ref, so_ref, small_ref, s_bufs)])
    s_ref[:] = jnp.zeros_like(s_ref)
    for l, (ga, gm) in enumerate(((sa0_ref, sm0_ref), (sa1_ref, sm1_ref))):
        base = l * SMALL // 2
        qk = unpermute_lanes(ga[:])
        for d in range(8):
            cols = slice(d * part, (d + 1) * part)
            s_ref[d, base:base + 2, :part] = qk[:2, cols]
            s_ref[d, base + 2:base + 6, :part] = ga[2:6, cols]
            s_ref[d, base + 6:base + 8, :part] = gm[5:7, cols]
            s_ref[d, base + 8:base + 9, :part] = gm[4:5, cols]
            for r in range(4):
                lo = d % 2 * GROUP + r * part
                s_ref[d, base + 9 + r:base + 10 + r, :part] = gm[d // 2:d // 2 + 1, lo:lo + part]
    for r in range(4):
        so_ref[pl.ds(r, 1)] = s_ref[pl.ds(job.chunk(r, 0), 1)]
    job.stage_one()
    job.stage_two()
    job.stage_three()
    job.stage_four()


def scatter_tail(g_a, *smalls):
    _, rows, model = g_a.shape
    wide = 2 * HEAD_DIM
    vmem = pl.BlockSpec(memory_space=pltpu.VMEM)
    n = rows // PIECE
    return pl.pallas_call(
        tail_kernel, in_specs=[pl.BlockSpec(memory_space=pl.ANY)] + [vmem] * 4, out_specs=[vmem] * 2,
        out_shape=[sds((rows, model), F32), sds((SMALL, wide), F32)],
        scratch_shapes=[pltpu.VMEM((4, rows, model), F32)] + scatter_bufs(n, PIECE, model)
        + [pltpu.VMEM((8, SMALL, wide), F32), pltpu.VMEM((4, SMALL, wide), F32)] + scatter_bufs(0, SMALL, wide)
        + scatter_sems(n + 1),
        compiler_params=pltpu.CompilerParams(collective_id=1, has_side_effects=True, vmem_limit_bytes=VMEM_BYTES),
        cost_estimate=cost(1e9, 8e6), name='scatter_tail',
    )(g_a, *smalls)


def finish_kernel(a0_ref, a1_ref, small_ref, m0_ref, m1_ref, ga_ref, gba_ref, gln_ref, gup_ref, gbu_ref, gdown_ref, gbd_ref):
    part, model = ga_ref.shape[2:]
    for l, (a_ref, m_ref) in enumerate(((a0_ref, m0_ref), (a1_ref, m1_ref))):
        for i in range(4):
            val = a_ref[i * part:(i + 1) * part, :]
            ga_ref[l, i] = unpermute_lanes(val) if i < 2 else val
            gup_ref[l, :, i * model:(i + 1) * model] = m_ref[i * part:(i + 1) * part, :]
        gdown_ref[l] = m_ref[4 * part:, :]
        base = l * SMALL // 2
        gba_ref[l] = small_ref[base:base + 4, :part]
        gln_ref[l] = small_ref[base + 4:base + 8, :part]
        gbd_ref[l:l + 1, :] = small_ref[base + 8:base + 9, :part]
        up = [small_ref[base + 9 + r:base + 10 + r, :part] for r in range(4)]
        gbu_ref[l:l + 1, :] = jnp.concatenate(up, axis=1)


def finish(shapes, *ins):
    vmem = pl.BlockSpec(memory_space=pltpu.VMEM)
    return pl.pallas_call(
        finish_kernel, in_specs=[vmem] * len(ins), out_specs=[vmem] * len(shapes), out_shape=shapes,
        compiler_params=pltpu.CompilerParams(vmem_limit_bytes=VMEM_BYTES), cost_estimate=cost(1e9, 6e6), name='finish',
    )(*ins)


def solution(mesh):
    axis = mesh.axis_names[0]
    batch_spec = P(axis)
    weight_specs = tuple(P(*([None] * k), axis) for k in (2, 2, 2, 1, 1, 1, 1))

    def gather(a):
        return lax.all_gather(a, axis, axis=0, tiled=False)

    def whole_step(x, lengths, d_y, *shards):
        model = x.shape[2]
        tables = rotary_tables(x.shape[1])
        tokens = (x.shape[0] * x.shape[1], model)
        head, vec0, vec1, attn_shard, mlp_shard0, mlp_shard1 = gather_head(*shards)
        vecs = (vec0, vec1)
        mlp_w0 = gather(mlp_shard0)
        attn_w = (head, gather(attn_shard))
        mlp_w = (mlp_w0, gather(mlp_shard1))

        hidden = x
        saved = []
        for l in range(2):
            *attn_saved, mid = attn_forward(lengths, hidden, attn_w[l], vecs[l], tables)
            mid2 = mid.reshape(tokens)
            y, act, slope = mlp_forward(mid2, mlp_w[l], vecs[l], FWD_ROWS)
            saved.append((hidden, attn_saved, mid2, act, slope))
            hidden = y.reshape(x.shape)

        grad = d_y.reshape(tokens)
        gw_attn, r_mlp, s_attn, s_mlp = None, {}, {}, {}
        for l in (1, 0):
            x_in, attn_saved, mid2, act, slope = saved[l]
            d_mid, gw_mlp, s_mlp[l], *done = mlp_backward(grad, mid2, act, slope, mlp_w[l], vecs[l], BWD_ROWS, gw_attn)
            r_mlp[l] = lax.psum_scatter(gw_mlp, axis, scatter_dimension=0, tiled=False)
            d_x, gw_attn, s_attn[l] = attn_backward(lengths, d_mid.reshape(x.shape), x_in, attn_saved, attn_w[l], vecs[l], tables)
            grad = d_x.reshape(tokens)
        a_sum0, small_sum = scatter_tail(gw_attn, s_attn[1], s_attn[0], s_mlp[1], s_mlp[0])
        shapes = [sds(s.shape, F32) for s in shards]
        outs = finish(shapes, a_sum0, *done, small_sum, r_mlp[0], r_mlp[1])
        return (d_x,) + tuple(outs)

    return jax.shard_map(whole_step, mesh=mesh,
                         in_specs=(batch_spec, batch_spec, batch_spec) + weight_specs,
                         out_specs=(batch_spec,) + weight_specs,
                         check_vma=False)
```

profile of v0, /device:TPU:0, one launch (start us, length us, event | category | flops | bytes accessed | tf_op | source)
XLA Modules:
  0.0 429.0 jit_solution(13092021322269339858)
XLA Ops:
  7.2 0.0 all-gather.7.cloned.1.call-start
  7.2 20.0 %gather_head.1 = (bf16[8,288,512]{2,1,0:T(8,128)(2,1)}, f32[16,512]{1,0:T(8,128)}, f32[16,512]{1,0:T(8,128)}, bf16[256,512]{1,0:T(8,128)(2,1)}, bf16[512,512]{1,0:T(8,128)(2,1)}, /*index=5*/bf16[512,512]{1,0:T(8,128)(2,1)}) custom-call(bf16[2,4,64,512]{3,2,1,0:T(8,128)(2,1)} %w_attn.1, bf16[2,4,64]{2,1,0:T(4,128)(2,1)} %b_attn.1, bf16[2,4,64]{2,1,0:T(4,128)(2,1)} %ln_par.1, ...), custom_call_target="tpu_custom_call" | custom-call | flops 1000000000 | bytes 4000000 | tf_op jit(solution)/shard_map/gather_head/pallas_call | solution.py:494
  27.2 0.0 all-gather.7.cloned.1.call-update
  27.3 0.0 all-gather.9.cloned.1.call-start
  27.3 0.7 all-gather.9.cloned.1.call-update
  28.0 0.0 all-gather.11.cloned.1.call-start
  28.1 0.7 all-gather.11.cloned.1.call-update
  28.8 0.0 reduce-scatter.3.cloned.1.call-start
  28.8 1.5 fusion
  30.3 34.2 %attn_fwd.2 = (bf16[8,384,512]{2,1,0:T(8,128)(2,1)}, bf16[8,384,512]{2,1,0:T(8,128)(2,1)}, bf16[8,384,512]{2,1,0:T(8,128)(2,1)}, bf16[8,384,3072]{2,1,0:T(8,128)...) custom-call(s32[8]{0:T(128)} %len_ref.7, bf16[8,384,512]{2,1,0:T(8,128)(2,1)} %x_ref.3, ...), custom_call_target="tpu_custom_call" | custom-call | flops 16000000000 | bytes 40000000 | tf_op jit(solution)/shard_map/attn_fwd/pallas_call | solution.py:298
  64.5 0.0 all-gather.7.cloned.1.call-done
  64.5 26.6 %mlp_fwd.2 = (bf16[3072,512]{1,0:T(8,128)(2,1)}, bf16[3072,2048]{1,0:T(8,128)(2,1)}, f32[3072,2048]{1,0:T(8,128)}) custom-call(bf16[3072,512]{1,0:T(8,128)(2,1)} %bitcast.21, bf16[8,512,512]{2,1,0:T(8,128)(2,1)} %bitcast.12, f32[16,512]{1,0:T(8,128)} %get-tuple-element.54.vec_ref), custom_call_target="tpu_custom_call" | custom-call | flops 12999999488 | bytes 50000000 | tf_op jit(solution)/shard_map/mlp_fwd/pallas_call | solution.py:311
  91.1 0.0 all-gather.9.cloned.1.call-done
  91.1 34.2 %attn_fwd.3 = (bf16[8,384,512]{2,1,0:T(8,128)(2,1)}, bf16[8,384,512]{2,1,0:T(8,128)(2,1)}, bf16[8,384,512]{2,1,0:T(8,128)(2,1)}, bf16[8,384,3072]{2,1,0:T(8,128)...) custom-call(s32[8]{0:T(128)} %len_ref.7, bf16[8,384,512]{2,1,0:T(8,128)(2,1)} %bitcast.24, ...), custom_call_target="tpu_custom_call" | custom-call | flops 16000000000 | bytes 40000000 | tf_op jit(solution)/shard_map/attn_fwd/pallas_call | solution.py:298
  125.3 0.0 all-gather.11.cloned.1.call-done
  125.3 26.4 %mlp_fwd.3 = (bf16[3072,512]{1,0:T(8,128)(2,1)}, bf16[3072,2048]{1,0:T(8,128)(2,1)}, f32[3072,2048]{1,0:T(8,128)}) custom-call(bf16[3072,512]{1,0:T(8,128)(2,1)} %bitcast.27, bf16[8,512,512]{2,1,0:T(8,128)(2,1)} %bitcast.14, f32[16,512]{1,0:T(8,128)} %get-tuple-element.59.vec_ref), custom_call_target="tpu_custom_call" | custom-call | flops 12999999488 | bytes 50000000 | tf_op jit(solution)/shard_map/mlp_fwd/pallas_call | solution.py:311
  151.7 38.6 %mlp_bwd.2 = (bf16[3072,512]{1,0:T(8,128)(2,1)}, f32[8,512,512]{2,1,0:T(8,128)}, f32[8,512]{1,0:T(8,128)}) custom-call(bf16[3072,512]{1,0:T(8,128)(2,1)} %bitcast.16, bf16[3072,512]{1,0:T(8,128)(2,1)} %bitcast.28, bf16[3072,2048]{1,0:T(8,128)(2,1)} %get-tuple-element.62.act_ref, f32[3072,2048]{1,0:T(8,128)} %get-tuple-element.63.slope_ref, ...), custom_call_target="tpu_custom_call" | custom-call | flops 25999998976 | bytes 60000000 | tf_op jit(solution)/shard_map/mlp_bwd/pallas_call | solution.py:335
  190.3 54.4 %attn_bwd.2 = (bf16[8,384,512]{2,1,0:T(8,128)(2,1)}, f32[8,256,512]{2,1,0:T(8,128)}, f32[8,512]{1,0:T(8,128)}) custom-call(s32[8]{0:T(128)} %len_ref.7, bf16[8,384,512]{2,1,0:T(8,128)(2,1)} %bitcast.29, bf16[8,384,512]{2,1,0:T(8,128)(2,1)} %bitcast.25, bf16[8,384,512]{2,1,0:T(8,128)(2,1)} %get-tuple-element.65.q_ref, ...), custom_call_target="tpu_custom_call" | custom-call | flops 30000001024 | bytes 50000000 | tf_op jit(solution)/shard_map/attn_bwd/pallas_call | solution.py:346
  244.8 40.8 %mlp_bwd.3 = (bf16[3072,512]{1,0:T(8,128)(2,1)}, f32[8,512,512]{2,1,0:T(8,128)}, f32[8,512]{1,0:T(8,128)}, f32[256,512]{1,0:T(8,128)}) custom-call(bf16[3072,512]{1,0:T(8,128)(2,1)} %bitcast.26, bf16[3072,512]{1,0:T(8,128)(2,1)} %bitcast.22, bf16[3072,2048]{1,0:T(8,128)(2,1)} %get-tuple-element.71.act_ref, f32[3072,2048]{1,0:T(8,128)} %get-tuple-element.72.slope_ref, ...), custom_call_target="tpu_custom_call" | custom-call | flops 25999998976 | bytes 60000000 | tf_op jit(solution)/shard_map/mlp_bwd/pallas_call | solution.py:335
  285.5 0.0 reduce-scatter.3.cloned.1.call-update
  285.6 0.0 reduce-scatter.5.cloned.1.call-start
  285.6 0.5 reduce-scatter.5.cloned.1.call-update
  286.1 53.9 %attn_bwd.3 = (bf16[8,384,512]{2,1,0:T(8,128)(2,1)}, f32[8,256,512]{2,1,0:T(8,128)}, f32[8,512]{1,0:T(8,128)}) custom-call(s32[8]{0:T(128)} %len_ref.7, bf16[8,384,512]{2,1,0:T(8,128)(2,1)} %bitcast.23, bf16[8,384,512]{2,1,0:T(8,128)(2,1)} %x_ref.3, bf16[8,384,512]{2,1,0:T(8,128)(2,1)} %get-tuple-element.75.q_ref, ...), custom_call_target="tpu_custom_call" | custom-call | flops 30000001024 | bytes 50000000 | tf_op jit(solution)/shard_map/attn_bwd/pallas_call | solution.py:346
  340.0 26.9 %scatter_tail.1 = (f32[256,512]{1,0:T(8,128)}, f32[32,128]{1,0:T(8,128)}) custom-call(f32[8,256,512]{2,1,0:T(8,128)} %get-tuple-element.81.ga_ref, f32[8,512]{1,0:T(8,128)} %get-tuple-element.82.sa1_ref, f32[8,512]{1,0:T(8,128)} %get-tuple-element.83.sa0_ref, f32[8,512]{1,0:T(8,128)} %get-tuple-element.84.sm1_ref, f32[8,512]{1,0:T(8,128)} %get-tuple-element.85.sm0_ref), custom_call_target="tpu_custom_call" | custom-call | flops 1000000000 | bytes 8000000 | tf_op jit(solution)/shard_map/scatter_tail/pallas_call | solution.py:618
  366.9 0.0 reduce-scatter.3.cloned.1.call-done
  366.9 51.3 %reduce-scatter.5.cloned.1.call-done = f32[1,512,512]{2,1,0:T(8,128)} async-done(((f32[8,512,512]{2,1,0:T(8,128)}), f32[1,512,512]{2,1,0:T(8,128)}) %reduce-scatter.5.cloned.1.call-update) | async-done | bytes 1048592 | tf_op jit(solution)/shard_map/reduce_scatter | solution.py:685
  418.2 4.0 finish.1
  (1 shorter events, 0.0 us)
Async XLA Ops:
  7.2 57.3 %all-gather.7.cloned.1.call-start = ((), (), s32[]{:S(2)}) async-start(), calls=%async_computation.4 | async-start | bytes 4718592 | tf_op jit(solution)/shard_map/all_gather | solution.py:659
  27.3 63.8 %all-gather.9.cloned.1.call-start = ((), (), s32[]{:S(2)}) async-start(), calls=%async_computation.5 | async-start | bytes 2359296 | tf_op jit(solution)/shard_map/all_gather | solution.py:659
  28.0 97.3 %all-gather.11.cloned.1.call-start = ((), (), s32[]{:S(2)}) async-start(), calls=%async_computation.6 | async-start | bytes 4718592 | tf_op jit(solution)/shard_map/all_gather | solution.py:659
  28.8 338.2 %reduce-scatter.3.cloned.1.call-start = ((), (), s32[]{:S(2)}) async-start(), calls=%async_computation.2 | async-start | bytes 9437184 | tf_op jit(solution)/shard_map/reduce_scatter | solution.py:685
  285.6 132.7 %reduce-scatter.5.cloned.1.call-start = ((), (), s32[]{:S(2)}) async-start(), calls=%async_computation.3 | async-start | bytes 9437184 | tf_op jit(solution)/shard_map/reduce_scatter | solution.py:685
Sparse Core Ops, SparseCore 0:
  27.4 31.0 all-gather.6
  60.3 22.2 all-gather.8
  84.4 31.0 all-gather.10
  285.7 65.8 reduce-scatter.2
  354.8 63.4 reduce-scatter.4
where the time goes:
time: 437 us; the launch traced here: 429 us
  Pallas kernels  360 us (82%)
  waiting for transfers between devices  53.3 us (12%)
  between operations  14 us (3%)
    pallas_call x2, Pallas kernels, attn_backward(): pl.pallas_call(attn_bwd_kernel, grid_spec=pltpu.PrefetchScalarGridSpec(nu...  108 us
    pallas_call x2, Pallas kernels, mlp_backward(): pl.pallas_call(kernel, grid=(tokens // rows,), in_specs=in_specs, out_spe...  79.4 us
    pallas_call x2, Pallas kernels, attn_forward(): pl.pallas_call(attn_fwd_kernel, grid_spec=pltpu.PrefetchScalarGridSpec(nu...  68.4 us
    pallas_call x2, Pallas kernels, mlp_forward(): pl.pallas_call(mlp_fwd_kernel, grid=(tokens // rows,), in_specs=[row_spec...  52.9 us
    reduce_scatter x2, waiting for transfers between devices, whole_step(): r_mlp[l] = lax.psum_scatter(gw_mlp, axis, scatter_dimension=0, tiled=False)  51.3 us
    pallas_call x1, Pallas kernels, scatter_tail(): pl.pallas_call(tail_kernel, in_specs=[pl.BlockSpec(memory_space=pl.ANY)]...  26.9 us
    pallas_call x1, Pallas kernels, gather_head(): pl.pallas_call(gather_kernel, in_specs=[vmem] * 7, out_specs=[vmem] * 6,...  20 us
  transfers between devices with their start and end apart: 5, of which 1 were waited for; matrix products, arithmetic and copies ran while one was open for 0% of the time, Pallas kernels for 41%

commit v1 on v0

--- a/solution.py
+++ b/solution.py
@@ -1,4 +1,5 @@
 import math
+import numpy as np
 import jax
 import jax.numpy as jnp
 from jax import lax
@@ -16,8 +17,9 @@
 GROUP = 256
 HEADS_GROUP = 4
 KEY_BLOCK = 128
+SEQS = 2
 FWD_ROWS = 384
-BWD_ROWS = 512
+BWD_ROWS = (512, 768)
 
 NN, NT, TN = (1, 0), (1, 1), (0, 0)
 
@@ -49,10 +51,11 @@
 
 def rotary_tables(seq_len):
     half_dim = HEAD_DIM // 2
-    freq_pos = (jnp.arange(2 * HEAD_DIM) % half_dim).astype(F32)
-    inv_freq = 1.0 / (THETA ** (freq_pos * (2.0 / HEAD_DIM)))
-    angles = jnp.arange(seq_len, dtype=F32)[:, None] * inv_freq[None, :]
-    return jnp.cos(angles), jnp.sin(angles)
+    freq_pos = (np.arange(2 * HEAD_DIM) % half_dim).astype(np.float32)
+    inv_freq = np.float32(1) / np.power(np.float32(THETA), freq_pos * np.float32(2 / HEAD_DIM))
+    angles = np.arange(seq_len, dtype=np.float32)[:, None] * inv_freq[None, :]
+    wide = angles.astype(np.float64)
+    return jnp.asarray(np.cos(wide).astype(np.float32)), jnp.asarray(np.sin(wide).astype(np.float32))
 
 
 def normalize(x_f32):
@@ -92,20 +95,32 @@
     return jnp.concatenate([block * m for m in masks], axis=0)
 
 
-def for_key_width(length, seq_len, body):
-    blocks = (length + KEY_BLOCK - 1) // KEY_BLOCK
-    for n in range(1, seq_len // KEY_BLOCK + 1):
-        @pl.when(blocks == n)
-        def _(n=n):
-            body(n * KEY_BLOCK)
+def each_sequence(len_ref, seq_len, body):
+    def one(i, carry):
+        length = len_ref[pl.program_id(0) * SEQS + i]
+        blocks = (length + KEY_BLOCK - 1) // KEY_BLOCK
+        for n in range(1, seq_len // KEY_BLOCK + 1):
+            @pl.when(blocks == n)
+            def _(n=n):
+                body(i, length, n * KEY_BLOCK)
+        return carry
+
+    lax.fori_loop(0, SEQS, one, 0)
+
+
+def flat(ref):
+    return ref[:].reshape(SEQS * ref.shape[1], ref.shape[2])
+
+
+def repeat_rows(table):
+    return jnp.concatenate([table[:]] * SEQS, axis=0)
 
 
 def attn_fwd_kernel(len_ref, x_ref, w_ref, vec_ref, cos_ref, sin_ref, q_ref, k_ref, v_ref, p_ref, ctx_ref, mid_ref):
     seq_len, model = x_ref.shape[1:]
-    length = len_ref[pl.program_id(0)]
-    x_hat, _ = normalize(x_ref[0].astype(F32))
+    x_hat, _ = normalize(flat(x_ref).astype(F32))
     h_one = (x_hat * line(vec_ref, 4) + line(vec_ref, 5)).astype(BF16)
-    cos_tab, sin_tab = cos_ref[:], sin_ref[:]
+    cos_tab, sin_tab = repeat_rows(cos_ref), repeat_rows(sin_ref)
     for i, out in enumerate((q_ref, k_ref)):
         proj = mm(h_one, square(w_ref, i)) + line(vec_ref, i)
         if i == 0:
@@ -113,31 +128,38 @@
         for g in range(model // GROUP):
             lo = g * GROUP
             first, second = rot_halves(*halves(proj, lo), cos_tab, sin_tab)
-            out[0, :, lo:lo + GROUP] = jnp.concatenate([first.astype(BF16), second.astype(BF16)], axis=1)
+            turned = jnp.concatenate([first.astype(BF16), second.astype(BF16)], axis=1)
+            out[:, :, lo:lo + GROUP] = turned.reshape(SEQS, seq_len, GROUP)
     proj = mm(h_one, square(w_ref, 2)) + line(vec_ref, 2)
-    v_ref[0] = proj.astype(BF16)
+    v_ref[:] = proj.astype(BF16).reshape(x_ref.shape)
     qk_masks, vo_masks = head_masks()
 
-    def attend(width):
+    def attend(b, length, width):
         valid = lax.broadcasted_iota(jnp.int32, (1, width), 1) < length
         for g in range(model // GROUP):
             lo = g * GROUP
-            k_cat = stack_masked(k_ref[0, 0:width, lo:lo + GROUP], qk_masks)
-            scores = mm(q_ref[0, :, lo:lo + GROUP], k_cat, NT)
+            k_cat = stack_masked(k_ref[b, :width, lo:lo + GROUP], qk_masks)
+            scores = mm(q_ref[b, :, lo:lo + GROUP], k_cat, NT)
             probs = []
             for h in range(HEADS_GROUP):
                 s_h = jnp.where(valid, scores[:, h * width:(h + 1) * width], NEG_BIG)
                 e_h = jnp.exp(s_h - jnp.max(s_h, axis=-1, keepdims=True))
                 p_h = (e_h * (1.0 / row_sum(e_h))).astype(BF16)
                 base = (g * HEADS_GROUP + h) * seq_len
-                p_ref[0, :, base:base + width] = p_h
+                p_ref[b, :, base:base + width] = p_h
                 probs.append(p_h)
-            v_cat = stack_masked(v_ref[0, 0:width, lo:lo + GROUP], vo_masks)
-            ctx_ref[0, :, lo:lo + GROUP] = mm(jnp.concatenate(probs, axis=1), v_cat).astype(BF16)
-
-    for_key_width(length, seq_len, attend)
-    attn_out = mm(ctx_ref[0], square(w_ref, 3))
-    mid_ref[0] = (x_ref[0].astype(F32) + attn_out + line(vec_ref, 3)).astype(BF16)
+            v_cat = stack_masked(v_ref[b, :width, lo:lo + GROUP], vo_masks)
+            ctx_ref[b, :, lo:lo + GROUP] = mm(jnp.concatenate(probs, axis=1), v_cat).astype(BF16)
+
+    each_sequence(len_ref, seq_len, attend)
+    attn_out = mm(flat(ctx_ref), square(w_ref, 3))
+    mid_ref[:] = (flat(x_ref).astype(F32) + attn_out + line(vec_ref, 3)).astype(BF16).reshape(x_ref.shape)
+
+
+def gelu_parts(pre):
+    cdf = 0.5 * lax.erf(pre * (1.0 / math.sqrt(2.0))) + 0.5
+    density = jnp.exp(pre * pre * -0.5) * (1.0 / math.sqrt(2.0 * math.pi))
+    return (pre * cdf).astype(BF16), cdf + pre * density
 
 
 def mlp_fwd_kernel(mid_ref, w_ref, vec_ref, y_ref, act_ref, slope_ref):
@@ -148,10 +170,7 @@
     for c in range(4):
         cols = slice(c * model, (c + 1) * model)
         pre = mm(h_two, square(w_ref, c)) + line(vec_ref, 9 + c)
-        cdf = 0.5 * lax.erf(pre * (1.0 / math.sqrt(2.0))) + 0.5
-        density = jnp.exp(pre * pre * -0.5) * (1.0 / math.sqrt(2.0 * math.pi))
-        act_ref[:, cols] = (pre * cdf).astype(BF16)
-        slope_ref[:, cols] = cdf + pre * density
+        act_ref[:, cols], slope_ref[:, cols] = gelu_parts(pre)
     out = mm(act_ref[:], w_ref[:, 256:512, :].reshape(4 * model, model))
     y_ref[:] = (mid + out + line(vec_ref, 8)).astype(BF16)
 
@@ -167,6 +186,10 @@
     pl.when(step == last)(job.stage_four)
 
 
+def mlp_last_kernel(dout_ref, mid_ref, w_ref, vec_ref, dmid_ref, gw_ref, gs_ref, dpre_ref, act_ref):
+    mlp_bwd_kernel(dout_ref, mid_ref, act_ref, None, w_ref, vec_ref, dmid_ref, gw_ref, gs_ref, dpre_ref)
+
+
 def mlp_bwd_kernel(dout_ref, mid_ref, act_ref, slope_ref, w_ref, vec_ref, dmid_ref, gw_ref, gs_ref, dpre_ref):
     model = mid_ref.shape[1]
 
@@ -182,7 +205,11 @@
     for c in range(4):
         cols = slice(c * model, (c + 1) * model)
         d_act = mm(d_out, w_ref[2 * c:2 * c + 2, 256:512, :].reshape(model, model), NT)
-        d_pre = d_act * slope_ref[:, cols]
+        if slope_ref is None:
+            act_ref[:, cols], slope = gelu_parts(mm(h_two, square(w_ref, c)) + line(vec_ref, 9 + c))
+        else:
+            slope = slope_ref[:, cols]
+        d_pre = d_act * slope
         add_line(gs_ref, c, d_pre)
         dpre_ref[:, cols] = d_pre.astype(BF16)
     for c in range(4):
@@ -201,48 +228,47 @@
 def attn_bwd_kernel(len_ref, dmid_ref, x_ref, q_ref, k_ref, v_ref, p_ref, ctx_ref, w_ref, vec_ref, cos_ref, sin_ref,
                     dx_ref, gw_ref, gs_ref, dctx_ref, dq_ref, dk_ref, dv_ref):
     seq_len, model = x_ref.shape[1:]
-    length = len_ref[pl.program_id(0)]
 
     @pl.when(pl.program_id(0) == 0)
     def _():
         gw_ref[:] = jnp.zeros_like(gw_ref)
         gs_ref[:] = jnp.zeros_like(gs_ref)
 
-    d_mid = dmid_ref[0]
+    d_mid = flat(dmid_ref)
     d_mid_f32 = d_mid.astype(F32)
     add_line(gs_ref, 3, d_mid_f32)
-    gw_ref[:, 192:256, :] += mm(ctx_ref[0], d_mid, TN).reshape(8, 64, model)
-    dctx_ref[:] = mm(d_mid, square(w_ref, 3), NT).astype(BF16)
+    gw_ref[:, 192:256, :] += mm(flat(ctx_ref), d_mid, TN).reshape(8, 64, model)
+    dctx_ref[:] = mm(d_mid, square(w_ref, 3), NT).astype(BF16).reshape(x_ref.shape)
     qk_masks, vo_masks = head_masks()
 
-    def attend(width):
+    def attend(b, length, width):
         for g in range(model // GROUP):
             lo = g * GROUP
-            d_ctx = dctx_ref[:, lo:lo + GROUP]
-            d_probs = mm(d_ctx, stack_masked(v_ref[0, 0:width, lo:lo + GROUP], vo_masks), NT)
+            d_ctx = dctx_ref[b, :, lo:lo + GROUP]
+            d_probs = mm(d_ctx, stack_masked(v_ref[b, :width, lo:lo + GROUP], vo_masks), NT)
             ds_list, dst_list, pt_list = [], [], []
             for h in range(HEADS_GROUP):
                 base = (g * HEADS_GROUP + h) * seq_len
-                p_bf = p_ref[0, :, base:base + width]
+                p_bf = p_ref[b, :, base:base + width]
                 p_h = p_bf.astype(F32)
                 dp_h = d_probs[:, h * width:(h + 1) * width]
                 ds_h = (p_h * (dp_h - row_sum(dp_h * p_h))).astype(BF16)
                 ds_list.append(ds_h)
                 dst_list.append(ds_h.T)
                 pt_list.append(p_bf.T)
-            k_cat = stack_masked(k_ref[0, 0:width, lo:lo + GROUP], qk_masks)
-            dq_ref[:, lo:lo + GROUP] = mm(jnp.concatenate(ds_list, axis=1), k_cat)
-            q_cat = stack_masked(q_ref[0, :, lo:lo + GROUP], qk_masks)
-            dk_ref[0:width, lo:lo + GROUP] = mm(jnp.concatenate(dst_list, axis=1), q_cat)
+            k_cat = stack_masked(k_ref[b, :width, lo:lo + GROUP], qk_masks)
+            dq_ref[b, :, lo:lo + GROUP] = mm(jnp.concatenate(ds_list, axis=1), k_cat)
+            q_cat = stack_masked(q_ref[b, :, lo:lo + GROUP], qk_masks)
+            dk_ref[b, :width, lo:lo + GROUP] = mm(jnp.concatenate(dst_list, axis=1), q_cat)
             do_cat = stack_masked(d_ctx, vo_masks)
-            dv_ref[0:width, lo:lo + GROUP] = mm(jnp.concatenate(pt_list, axis=1), do_cat)
+            dv_ref[b, :width, lo:lo + GROUP] = mm(jnp.concatenate(pt_list, axis=1), do_cat)
         if width < seq_len:
-            dk_ref[width:, :] = jnp.zeros((seq_len - width, model), F32)
-            dv_ref[width:, :] = jnp.zeros((seq_len - width, model), F32)
-
-    for_key_width(length, seq_len, attend)
-    cos_tab, sin_tab = cos_ref[:], sin_ref[:]
-    x_hat, rstd = normalize(x_ref[0].astype(F32))
+            dk_ref[b, width:, :] = jnp.zeros((seq_len - width, model), F32)
+            dv_ref[b, width:, :] = jnp.zeros((seq_len - width, model), F32)
+
+    each_sequence(len_ref, seq_len, attend)
+    cos_tab, sin_tab = repeat_rows(cos_ref), repeat_rows(sin_ref)
+    x_hat, rstd = normalize(flat(x_ref).astype(F32))
     h_one = (x_hat * line(vec_ref, 4) + line(vec_ref, 5)).astype(BF16)
     d_h = None
     for i, src in enumerate((dq_ref, dk_ref, dv_ref)):
@@ -250,12 +276,12 @@
             pieces = []
             for g in range(model // GROUP):
                 lo = g * GROUP
-                pieces.extend(unrot_halves(*halves(src, lo), cos_tab, sin_tab))
+                pieces.extend(unrot_halves(*halves(flat(src), lo), cos_tab, sin_tab))
             d_proj = jnp.concatenate(pieces, axis=1)
             if i == 0:
                 d_proj = d_proj * (HEAD_DIM ** -0.5)
         else:
-            d_proj = src[:]
+            d_proj = flat(src)
         d_proj = d_proj.astype(BF16)
         add_line(gs_ref, i, d_proj.astype(F32))
         gw_ref[:, i * 64:(i + 1) * 64, :] += mm(h_one, d_proj, TN).reshape(8, 64, model)
@@ -263,11 +289,11 @@
         d_h = part if d_h is None else d_h + part
     add_line(gs_ref, 4, d_h * x_hat)
     add_line(gs_ref, 5, d_h)
-    dx_ref[0] = (d_mid_f32 + norm_bwd(d_h, x_hat, rstd, line(vec_ref, 4))).astype(BF16)
+    dx_ref[:] = (d_mid_f32 + norm_bwd(d_h, x_hat, rstd, line(vec_ref, 4))).astype(BF16).reshape(x_ref.shape)
 
 
 def seq_spec(*tail):
-    return pl.BlockSpec((1,) + tail, lambda b, *_: (b,) + (0,) * len(tail))
+    return pl.BlockSpec((SEQS,) + tail, lambda b, *_: (b,) + (0,) * len(tail))
 
 
 def row_spec(rows, cols):
@@ -298,7 +324,7 @@
     return pl.pallas_call(
         attn_fwd_kernel,
         grid_spec=pltpu.PrefetchScalarGridSpec(
-            num_scalar_prefetch=1, grid=(n,),
+            num_scalar_prefetch=1, grid=(n // SEQS,),
             in_specs=[spec, whole((8, 256, model)), whole(vec.shape), whole(tables[0].shape), whole(tables[1].shape)],
             out_specs=[spec, spec, spec, seq_spec(seq_len, heads * seq_len), spec, spec]),
         out_shape=[act, act, act, sds((n, seq_len, heads * seq_len), BF16), act, act],
@@ -325,6 +351,9 @@
     out_shape = [sds(mid.shape, BF16), sds(w.shape, F32), sds((8, model), F32)]
     scratch = [pltpu.VMEM((rows, 4 * model), BF16)]
     ins, kernel, extra = (d_out, mid, act, slope, w, vec), mlp_bwd_kernel, {}
+    if act is None:
+        ins, kernel, in_specs = (d_out, mid, w, vec), mlp_last_kernel, in_specs[:2] + in_specs[4:]
+        scratch = scratch + scratch
     if g_a is not None:
         ins, kernel, extra = ins + (g_a,), mlp_bwd_scatter_kernel, {'collective_id': 2, 'has_side_effects': True}
         in_specs.append(pl.BlockSpec(memory_space=pl.ANY))
@@ -346,11 +375,11 @@
     return pl.pallas_call(
         attn_bwd_kernel,
         grid_spec=pltpu.PrefetchScalarGridSpec(
-            num_scalar_prefetch=1, grid=(n,),
+            num_scalar_prefetch=1, grid=(n // SEQS,),
             in_specs=[spec, spec, spec, spec, spec, seq_spec(seq_len, heads * seq_len), spec, whole((8, 256, model)),
                       whole(vec.shape), whole(tables[0].shape), whole(tables[1].shape)],
             out_specs=[spec, whole((8, 256, model)), whole((8, model))],
-            scratch_shapes=[pltpu.VMEM((seq_len, model), BF16)] + [pltpu.VMEM((seq_len, model), F32)] * 3),
+            scratch_shapes=[pltpu.VMEM((SEQS, seq_len, model), t) for t in (BF16, F32, F32, F32)]),
         out_shape=[sds(x.shape, BF16), sds((8, 256, model), F32), sds((8, model), F32)],
         compiler_params=params(), cost_estimate=cost(30e9, 50e6), name='attn_bwd',
     )(lengths, d_mid, x, *saved, w, vec, *tables)
@@ -461,11 +490,6 @@
     for copy in (x_soon, y_soon, x_late, y_late, c_one, c_two):
         copy.start()
     out_ref[pl.ds(me, 1)] = pack_ref[:][None]
-    pack_attn(put_second, w_attn[1], perm)
-    for l, mlp_ref in enumerate((mlp0_ref, mlp1_ref)):
-        for c in range(4):
-            mlp_ref[c * part:(c + 1) * part, :] = w_up[l, :, c * model:(c + 1) * model]
-        mlp_ref[4 * part:, :] = w_down[l]
     on_x, on_y = pass_on(py, top, px), pass_on(px, low, py)
     steps = [(y_soon, on_x, pass_on(py, top, core)), (x_soon, on_y, pass_on(px, low, core)),
              (x_late, None, pass_on(px, top, core)), (y_late, None, pass_on(py, low, core)),
@@ -475,6 +499,11 @@
         if onward:
             onward.start()
         across.start()
+    pack_attn(put_second, w_attn[1], perm)
+    for l, mlp_ref in enumerate((mlp0_ref, mlp1_ref)):
+        for c in range(4):
+            mlp_ref[c * part:(c + 1) * part, :] = w_up[l, :, c * model:(c + 1) * model]
+        mlp_ref[4 * part:, :] = w_down[l]
     from_core = [c_one, c_two] + [across for _, _, across in steps]
     for copy in from_core:
         copy.wait_recv()
@@ -673,7 +702,9 @@
         for l in range(2):
             *attn_saved, mid = attn_forward(lengths, hidden, attn_w[l], vecs[l], tables)
             mid2 = mid.reshape(tokens)
-            y, act, slope = mlp_forward(mid2, mlp_w[l], vecs[l], FWD_ROWS)
+            act = slope = None
+            if l == 0:
+                y, act, slope = mlp_forward(mid2, mlp_w[l], vecs[l], FWD_ROWS)
             saved.append((hidden, attn_saved, mid2, act, slope))
             hidden = y.reshape(x.shape)
 
@@ -681,7 +712,7 @@
         gw_attn, r_mlp, s_attn, s_mlp = None, {}, {}, {}
         for l in (1, 0):
             x_in, attn_saved, mid2, act, slope = saved[l]
-            d_mid, gw_mlp, s_mlp[l], *done = mlp_backward(grad, mid2, act, slope, mlp_w[l], vecs[l], BWD_ROWS, gw_attn)
+            d_mid, gw_mlp, s_mlp[l], *done = mlp_backward(grad, mid2, act, slope, mlp_w[l], vecs[l], BWD_ROWS[l], gw_attn)
             r_mlp[l] = lax.psum_scatter(gw_mlp, axis, scatter_dimension=0, tiled=False)
             d_x, gw_attn, s_attn[l] = attn_backward(lengths, d_mid.reshape(x.shape), x_in, attn_saved, attn_w[l], vecs[l], tables)
             grad = d_x.reshape(tokens)

time: 437 us -> 416 us (0.952)
  Pallas kernels: 360 us -> 338 us
    pallas_call x2 -> x1, Pallas kernels: 52.9 us -> 26.5 us  [mlp_forward(): pl.pallas_call(mlp_fwd_kernel, grid=(tokens // rows,), in_specs=[row_spec...]
    pallas_call x2, Pallas kernels: 79.4 us -> 87.2 us  [mlp_backward(): pl.pallas_call(kernel, grid=(tokens // rows,), in_specs=in_specs, out_spe...]
    pallas_call x2, Pallas kernels: 108 us -> 103 us  [attn_backward(): pl.pallas_call(attn_bwd_kernel, grid_spec=pltpu.PrefetchScalarGridSpec(nu...]
  transfers between devices with their start and end apart: 5 -> 5, of which waited for: 1 -> 1; matrix products, arithmetic and copies ran while one was open for 0% -> 0% of each run, Pallas kernels for 41% -> 43%
where the time goes in v1:
time: 416 us; the launch traced here: 408 us
  Pallas kernels  338 us (81%)
  waiting for transfers between devices  55.6 us (13%)
  between operations  14.2 us (3%)
    pallas_call x2, Pallas kernels, attn_backward(): pl.pallas_call(attn_bwd_kernel, grid_spec=pltpu.PrefetchScalarGridSpec(nu...  103 us
    pallas_call x2, Pallas kernels, mlp_backward(): pl.pallas_call(kernel, grid=(tokens // rows,), in_specs=in_specs, out_spe...  87.2 us
    pallas_call x2, Pallas kernels, attn_forward(): pl.pallas_call(attn_fwd_kernel, grid_spec=pltpu.PrefetchScalarGridSpec(nu...  67.6 us
    reduce_scatter x2, waiting for transfers between devices, whole_step(): r_mlp[l] = lax.psum_scatter(gw_mlp, axis, scatter_dimension=0, tiled=False)  53.7 us
    pallas_call x1, Pallas kernels, scatter_tail(): pl.pallas_call(tail_kernel, in_specs=[pl.BlockSpec(memory_space=pl.ANY)]...  29.4 us
    pallas_call x1, Pallas kernels, mlp_forward(): pl.pallas_call(mlp_fwd_kernel, grid=(tokens // rows,), in_specs=[row_spec...  26.5 us
    pallas_call x1, Pallas kernels, gather_head(): pl.pallas_call(gather_kernel, in_specs=[vmem] * 7, out_specs=[vmem] * 6,...  19.9 us
  transfers between devices with their start and end apart: 5, of which 1 were waited for; matrix products, arithmetic and copies ran while one was open for 0% of the time, Pallas kernels for 43%

profile of v1, /device:TPU:0, one launch (start us, length us, event | category | flops | bytes accessed | tf_op | source)
XLA Modules:
  0.0 408.0 jit_solution(12901928421570261163)
XLA Ops:
  7.2 0.0 all-gather.7.cloned.1.call-start
  7.2 19.9 %gather_head.1 = (bf16[8,288,512]{2,1,0:T(8,128)(2,1)}, f32[16,512]{1,0:T(8,128)}, f32[16,512]{1,0:T(8,128)}, bf16[256,512]{1,0:T(8,128)(2,1)}, bf16[512,512]{1,0:T(8,128)(2,1)}, /*index=5*/bf16[512,512]{1,0:T(8,128)(2,1)}) custom-call(bf16[2,4,64,512]{3,2,1,0:T(8,128)(2,1)} %w_attn.1, bf16[2,4,64]{2,1,0:T(4,128)(2,1)} %b_attn.1, bf16[2,4,64]{2,1,0:T(4,128)(2,1)} %ln_par.1, ...), custom_call_target="tpu_custom_call" | custom-call | flops 1000000000 | bytes 4000000 | tf_op jit(solution)/shard_map/gather_head/pallas_call | solution.py:523
  27.2 0.0 all-gather.7.cloned.1.call-update
  27.2 0.0 all-gather.9.cloned.1.call-start
  27.2 0.7 all-gather.9.cloned.1.call-update
  27.9 0.0 all-gather.11.cloned.1.call-start
  28.0 0.7 all-gather.11.cloned.1.call-update
  28.7 0.0 reduce-scatter.3.cloned.1.call-start
  28.7 33.8 %attn_fwd.2 = (bf16[8,384,512]{2,1,0:T(8,128)(2,1)}, bf16[8,384,512]{2,1,0:T(8,128)(2,1)}, bf16[8,384,512]{2,1,0:T(8,128)(2,1)}, bf16[8,384,3072]{2,1,0:T(8,128)...) custom-call(s32[8]{0:T(128)} %len_ref.7, bf16[8,384,512]{2,1,0:T(8,128)(2,1)} %x_ref.3, ...), custom_call_target="tpu_custom_call" | custom-call | flops 16000000000 | bytes 40000000 | tf_op jit(solution)/shard_map/attn_fwd/pallas_call | solution.py:324
  62.5 0.0 all-gather.7.cloned.1.call-done
  62.5 26.5 %mlp_fwd.1 = (bf16[3072,512]{1,0:T(8,128)(2,1)}, bf16[3072,2048]{1,0:T(8,128)(2,1)}, f32[3072,2048]{1,0:T(8,128)}) custom-call(bf16[3072,512]{1,0:T(8,128)(2,1)} %bitcast.20, bf16[8,512,512]{2,1,0:T(8,128)(2,1)} %bitcast.12, f32[16,512]{1,0:T(8,128)} %get-tuple-element.52.vec_ref), custom_call_target="tpu_custom_call" | custom-call | flops 12999999488 | bytes 50000000 | tf_op jit(solution)/shard_map/mlp_fwd/pallas_call | solution.py:337
  89.0 0.0 all-gather.9.cloned.1.call-done
  89.0 33.9 %attn_fwd.3 = (bf16[8,384,512]{2,1,0:T(8,128)(2,1)}, bf16[8,384,512]{2,1,0:T(8,128)(2,1)}, bf16[8,384,512]{2,1,0:T(8,128)(2,1)}, bf16[8,384,3072]{2,1,0:T(8,128)...) custom-call(s32[8]{0:T(128)} %len_ref.7, bf16[8,384,512]{2,1,0:T(8,128)(2,1)} %bitcast.23, ...), custom_call_target="tpu_custom_call" | custom-call | flops 16000000000 | bytes 40000000 | tf_op jit(solution)/shard_map/attn_fwd/pallas_call | solution.py:324
  122.9 0.0 all-gather.11.cloned.1.call-done
  122.9 46.8 %mlp_bwd.2 = (bf16[3072,512]{1,0:T(8,128)(2,1)}, f32[8,512,512]{2,1,0:T(8,128)}, f32[8,512]{1,0:T(8,128)}) custom-call(bf16[3072,512]{1,0:T(8,128)(2,1)} %bitcast.15, bf16[3072,512]{1,0:T(8,128)(2,1)} %bitcast.27, bf16[8,512,512]{2,1,0:T(8,128)(2,1)} %bitcast.14, f32[16,512]{1,0:T(8,128)} %get-tuple-element.57.vec_ref), custom_call_target="tpu_custom_call" | custom-call | flops 25999998976 | bytes 60000000 | tf_op jit(solution)/shard_map/mlp_bwd/pallas_call | solution.py:364
  169.7 51.8 %attn_bwd.2 = (bf16[8,384,512]{2,1,0:T(8,128)(2,1)}, f32[8,256,512]{2,1,0:T(8,128)}, f32[8,512]{1,0:T(8,128)}) custom-call(s32[8]{0:T(128)} %len_ref.7, bf16[8,384,512]{2,1,0:T(8,128)(2,1)} %bitcast.26, bf16[8,384,512]{2,1,0:T(8,128)(2,1)} %bitcast.24, bf16[8,384,512]{2,1,0:T(8,128)(2,1)} %get-tuple-element.61.q_ref, ...), custom_call_target="tpu_custom_call" | custom-call | flops 30000001024 | bytes 50000000 | tf_op jit(solution)/shard_map/attn_bwd/pallas_call | solution.py:375
  221.6 40.4 %mlp_bwd.3 = (bf16[3072,512]{1,0:T(8,128)(2,1)}, f32[8,512,512]{2,1,0:T(8,128)}, f32[8,512]{1,0:T(8,128)}, f32[256,512]{1,0:T(8,128)}) custom-call(bf16[3072,512]{1,0:T(8,128)(2,1)} %bitcast.25, bf16[3072,512]{1,0:T(8,128)(2,1)} %bitcast.21, bf16[3072,2048]{1,0:T(8,128)(2,1)} %get-tuple-element.67.act_ref, f32[3072,2048]{1,0:T(8,128)} %get-tuple-element.68.slope_ref, ...), custom_call_target="tpu_custom_call" | custom-call | flops 25999998976 | bytes 60000000 | tf_op jit(solution)/shard_map/mlp_bwd/pallas_call | solution.py:364
  262.0 0.0 reduce-scatter.3.cloned.1.call-update
  262.0 0.0 reduce-scatter.5.cloned.1.call-start
  262.1 0.5 reduce-scatter.5.cloned.1.call-update
  262.6 51.3 %attn_bwd.3 = (bf16[8,384,512]{2,1,0:T(8,128)(2,1)}, f32[8,256,512]{2,1,0:T(8,128)}, f32[8,512]{1,0:T(8,128)}) custom-call(s32[8]{0:T(128)} %len_ref.7, bf16[8,384,512]{2,1,0:T(8,128)(2,1)} %bitcast.22, bf16[8,384,512]{2,1,0:T(8,128)(2,1)} %x_ref.3, bf16[8,384,512]{2,1,0:T(8,128)(2,1)} %get-tuple-element.71.q_ref, ...), custom_call_target="tpu_custom_call" | custom-call | flops 30000001024 | bytes 50000000 | tf_op jit(solution)/shard_map/attn_bwd/pallas_call | solution.py:375
  313.9 29.4 %scatter_tail.1 = (f32[256,512]{1,0:T(8,128)}, f32[32,128]{1,0:T(8,128)}) custom-call(f32[8,256,512]{2,1,0:T(8,128)} %get-tuple-element.77.ga_ref, f32[8,512]{1,0:T(8,128)} %get-tuple-element.78.sa1_ref, f32[8,512]{1,0:T(8,128)} %get-tuple-element.79.sa0_ref, f32[8,512]{1,0:T(8,128)} %get-tuple-element.80.sm1_ref, f32[8,512]{1,0:T(8,128)} %get-tuple-element.81.sm0_ref), custom_call_target="tpu_custom_call" | custom-call | flops 1000000000 | bytes 8000000 | tf_op jit(solution)/shard_map/scatter_tail/pallas_call | solution.py:647
  343.4 0.0 reduce-scatter.3.cloned.1.call-done
  343.4 53.6 %reduce-scatter.5.cloned.1.call-done = f32[1,512,512]{2,1,0:T(8,128)} async-done(((f32[8,512,512]{2,1,0:T(8,128)}), f32[1,512,512]{2,1,0:T(8,128)}) %reduce-scatter.5.cloned.1.call-update) | async-done | bytes 1048592 | tf_op jit(solution)/shard_map/reduce_scatter | solution.py:716
  397.0 4.0 finish.1
Async XLA Ops:
  7.2 55.3 %all-gather.7.cloned.1.call-start = ((), (), s32[]{:S(2)}) async-start(), calls=%async_computation.4 | async-start | bytes 4718592 | tf_op jit(solution)/shard_map/all_gather | solution.py:688
  27.2 61.8 %all-gather.9.cloned.1.call-start = ((), (), s32[]{:S(2)}) async-start(), calls=%async_computation.5 | async-start | bytes 2359296 | tf_op jit(solution)/shard_map/all_gather | solution.py:688
  27.9 94.9 %all-gather.11.cloned.1.call-start = ((), (), s32[]{:S(2)}) async-start(), calls=%async_computation.6 | async-start | bytes 4718592 | tf_op jit(solution)/shard_map/all_gather | solution.py:688
  28.7 314.7 %reduce-scatter.3.cloned.1.call-start = ((), (), s32[]{:S(2)}) async-start(), calls=%async_computation.2 | async-start | bytes 9437184 | tf_op jit(solution)/shard_map/reduce_scatter | solution.py:716
  262.0 135.0 %reduce-scatter.5.cloned.1.call-start = ((), (), s32[]{:S(2)}) async-start(), calls=%async_computation.3 | async-start | bytes 9437184 | tf_op jit(solution)/shard_map/reduce_scatter | solution.py:716
Sparse Core Ops, SparseCore 0:
  27.3 31.0 all-gather.6
  60.3 22.1 all-gather.8
  84.3 31.0 all-gather.10
  262.1 68.3 reduce-scatter.2
  333.7 63.2 reduce-scatter.4

commit v2 on v1

--- a/solution.py
+++ b/solution.py
@@ -135,14 +135,19 @@
     qk_masks, vo_masks = head_masks()
 
     def attend(b, length, width):
-        valid = lax.broadcasted_iota(jnp.int32, (1, width), 1) < length
-        for g in range(model // GROUP):
+        open_keys = width - KEY_BLOCK
+        valid = lax.broadcasted_iota(jnp.int32, (1, KEY_BLOCK), 1) < length - open_keys
+        all_scores = []
+        for lo in range(0, model, GROUP):
+            k_cat = stack_masked(k_ref[b, :width, lo:lo + GROUP], qk_masks)
+            all_scores.append(mm(q_ref[b, :, lo:lo + GROUP], k_cat, NT))
+        for g, scores in enumerate(all_scores):
             lo = g * GROUP
-            k_cat = stack_masked(k_ref[b, :width, lo:lo + GROUP], qk_masks)
-            scores = mm(q_ref[b, :, lo:lo + GROUP], k_cat, NT)
             probs = []
             for h in range(HEADS_GROUP):
-                s_h = jnp.where(valid, scores[:, h * width:(h + 1) * width], NEG_BIG)
+                s_h = scores[:, h * width:(h + 1) * width]
+                last = jnp.where(valid, s_h[:, open_keys:], NEG_BIG)
+                s_h = jnp.concatenate([s_h[:, :open_keys], last], axis=1) if open_keys else last
                 e_h = jnp.exp(s_h - jnp.max(s_h, axis=-1, keepdims=True))
                 p_h = (e_h * (1.0 / row_sum(e_h))).astype(BF16)
                 base = (g * HEADS_GROUP + h) * seq_len
@@ -242,10 +247,12 @@
     qk_masks, vo_masks = head_masks()
 
     def attend(b, length, width):
-        for g in range(model // GROUP):
+        all_dp = []
+        for lo in range(0, model, GROUP):
+            all_dp.append(mm(dctx_ref[b, :, lo:lo + GROUP], stack_masked(v_ref[b, :width, lo:lo + GROUP], vo_masks), NT))
+        for g, d_probs in enumerate(all_dp):
             lo = g * GROUP
             d_ctx = dctx_ref[b, :, lo:lo + GROUP]
-            d_probs = mm(d_ctx, stack_masked(v_ref[b, :width, lo:lo + GROUP], vo_masks), NT)
             ds_list, dst_list, pt_list = [], [], []
             for h in range(HEADS_GROUP):
                 base = (g * HEADS_GROUP + h) * seq_len

time: 416 us -> 419 us (level)
    pallas_call x2, Pallas kernels: 103 us -> 114 us  [attn_backward(): pl.pallas_call(attn_bwd_kernel, grid_spec=pltpu.PrefetchScalarGridSpec(nu...]
    pallas_call x2, Pallas kernels: 67.6 us -> 60.4 us  [attn_forward(): pl.pallas_call(attn_fwd_kernel, grid_spec=pltpu.PrefetchScalarGridSpec(nu...]
  transfers between devices with their start and end apart: 5 -> 5, of which waited for: 1 -> 1; matrix products, arithmetic and copies ran while one was open for 0% -> 0% of each run, Pallas kernels for 43% -> 41%
where the time goes in v2:
time: 419 us; the launch traced here: 412 us
  Pallas kernels  341 us (81%)
  waiting for transfers between devices  56.3 us (13%)
  between operations  14.2 us (3%)
    pallas_call x2, Pallas kernels, attn_backward(): pl.pallas_call(attn_bwd_kernel, grid_spec=pltpu.PrefetchScalarGridSpec(nu...  114 us
    pallas_call x2, Pallas kernels, mlp_backward(): pl.pallas_call(kernel, grid=(tokens // rows,), in_specs=in_specs, out_spe...  87.6 us
    pallas_call x2, Pallas kernels, attn_forward(): pl.pallas_call(attn_fwd_kernel, grid_spec=pltpu.PrefetchScalarGridSpec(nu...  60.4 us
    reduce_scatter x2, waiting for transfers between devices, whole_step(): r_mlp[l] = lax.psum_scatter(gw_mlp, axis, scatter_dimension=0, tiled=False)  54.4 us
    pallas_call x1, Pallas kernels, scatter_tail(): pl.pallas_call(tail_kernel, in_specs=[pl.BlockSpec(memory_space=pl.ANY)]...  29.3 us
    pallas_call x1, Pallas kernels, mlp_forward(): pl.pallas_call(mlp_fwd_kernel, grid=(tokens // rows,), in_specs=[row_spec...  26.3 us
    pallas_call x1, Pallas kernels, gather_head(): pl.pallas_call(gather_kernel, in_specs=[vmem] * 7, out_specs=[vmem] * 6,...  19.9 us
  transfers between devices with their start and end apart: 5, of which 1 were waited for; matrix products, arithmetic and copies ran while one was open for 0% of the time, Pallas kernels for 41%

profile of v2, /device:TPU:0, one launch (start us, length us, event | category | flops | bytes accessed | tf_op | source)
XLA Modules:
  0.0 411.9 jit_solution(3001889990245611039)
XLA Ops:
  7.2 0.0 all-gather.7.cloned.1.call-start
  7.2 19.9 %gather_head.1 = (bf16[8,288,512]{2,1,0:T(8,128)(2,1)}, f32[16,512]{1,0:T(8,128)}, f32[16,512]{1,0:T(8,128)}, bf16[256,512]{1,0:T(8,128)(2,1)}, bf16[512,512]{1,0:T(8,128)(2,1)}, /*index=5*/bf16[512,512]{1,0:T(8,128)(2,1)}) custom-call(bf16[2,4,64,512]{3,2,1,0:T(8,128)(2,1)} %w_attn.1, bf16[2,4,64]{2,1,0:T(4,128)(2,1)} %b_attn.1, bf16[2,4,64]{2,1,0:T(4,128)(2,1)} %ln_par.1, ...), custom_call_target="tpu_custom_call" | custom-call | flops 1000000000 | bytes 4000000 | tf_op jit(solution)/shard_map/gather_head/pallas_call | solution.py:530
  27.2 0.0 all-gather.7.cloned.1.call-update
  27.2 0.0 all-gather.9.cloned.1.call-start
  27.2 0.7 all-gather.9.cloned.1.call-update
  27.9 0.0 all-gather.11.cloned.1.call-start
  28.0 0.7 all-gather.11.cloned.1.call-update
  28.7 0.0 reduce-scatter.3.cloned.1.call-start
  28.7 30.1 %attn_fwd.2 = (bf16[8,384,512]{2,1,0:T(8,128)(2,1)}, bf16[8,384,512]{2,1,0:T(8,128)(2,1)}, bf16[8,384,512]{2,1,0:T(8,128)(2,1)}, bf16[8,384,3072]{2,1,0:T(8,128)...) custom-call(s32[8]{0:T(128)} %len_ref.7, bf16[8,384,512]{2,1,0:T(8,128)(2,1)} %x_ref.3, ...), custom_call_target="tpu_custom_call" | custom-call | flops 16000000000 | bytes 40000000 | tf_op jit(solution)/shard_map/attn_fwd/pallas_call | solution.py:331
  58.9 0.0 all-gather.7.cloned.1.call-done
  58.9 26.3 %mlp_fwd.1 = (bf16[3072,512]{1,0:T(8,128)(2,1)}, bf16[3072,2048]{1,0:T(8,128)(2,1)}, f32[3072,2048]{1,0:T(8,128)}) custom-call(bf16[3072,512]{1,0:T(8,128)(2,1)} %bitcast.20, bf16[8,512,512]{2,1,0:T(8,128)(2,1)} %bitcast.12, f32[16,512]{1,0:T(8,128)} %get-tuple-element.52.vec_ref), custom_call_target="tpu_custom_call" | custom-call | flops 12999999488 | bytes 50000000 | tf_op jit(solution)/shard_map/mlp_fwd/pallas_call | solution.py:344
  85.2 0.0 all-gather.9.cloned.1.call-done
  85.2 30.3 %attn_fwd.3 = (bf16[8,384,512]{2,1,0:T(8,128)(2,1)}, bf16[8,384,512]{2,1,0:T(8,128)(2,1)}, bf16[8,384,512]{2,1,0:T(8,128)(2,1)}, bf16[8,384,3072]{2,1,0:T(8,128)...) custom-call(s32[8]{0:T(128)} %len_ref.7, bf16[8,384,512]{2,1,0:T(8,128)(2,1)} %bitcast.23, ...), custom_call_target="tpu_custom_call" | custom-call | flops 16000000000 | bytes 40000000 | tf_op jit(solution)/shard_map/attn_fwd/pallas_call | solution.py:331
  115.5 0.0 all-gather.11.cloned.1.call-done
  115.5 46.7 %mlp_bwd.2 = (bf16[3072,512]{1,0:T(8,128)(2,1)}, f32[8,512,512]{2,1,0:T(8,128)}, f32[8,512]{1,0:T(8,128)}) custom-call(bf16[3072,512]{1,0:T(8,128)(2,1)} %bitcast.15, bf16[3072,512]{1,0:T(8,128)(2,1)} %bitcast.27, bf16[8,512,512]{2,1,0:T(8,128)(2,1)} %bitcast.14, f32[16,512]{1,0:T(8,128)} %get-tuple-element.57.vec_ref), custom_call_target="tpu_custom_call" | custom-call | flops 25999998976 | bytes 60000000 | tf_op jit(solution)/shard_map/mlp_bwd/pallas_call | solution.py:371
  162.2 62.5 %attn_bwd.2 = (bf16[8,384,512]{2,1,0:T(8,128)(2,1)}, f32[8,256,512]{2,1,0:T(8,128)}, f32[8,512]{1,0:T(8,128)}) custom-call(s32[8]{0:T(128)} %len_ref.7, bf16[8,384,512]{2,1,0:T(8,128)(2,1)} %bitcast.26, bf16[8,384,512]{2,1,0:T(8,128)(2,1)} %bitcast.24, bf16[8,384,512]{2,1,0:T(8,128)(2,1)} %get-tuple-element.61.q_ref, ...), custom_call_target="tpu_custom_call" | custom-call | flops 30000001024 | bytes 50000000 | tf_op jit(solution)/shard_map/attn_bwd/pallas_call | solution.py:382
  224.8 40.8 %mlp_bwd.3 = (bf16[3072,512]{1,0:T(8,128)(2,1)}, f32[8,512,512]{2,1,0:T(8,128)}, f32[8,512]{1,0:T(8,128)}, f32[256,512]{1,0:T(8,128)}) custom-call(bf16[3072,512]{1,0:T(8,128)(2,1)} %bitcast.25, bf16[3072,512]{1,0:T(8,128)(2,1)} %bitcast.21, bf16[3072,2048]{1,0:T(8,128)(2,1)} %get-tuple-element.67.act_ref, f32[3072,2048]{1,0:T(8,128)} %get-tuple-element.68.slope_ref, ...), custom_call_target="tpu_custom_call" | custom-call | flops 25999998976 | bytes 60000000 | tf_op jit(solution)/shard_map/mlp_bwd/pallas_call | solution.py:371
  265.6 0.0 reduce-scatter.3.cloned.1.call-update
  265.7 0.0 reduce-scatter.5.cloned.1.call-start
  265.7 0.5 reduce-scatter.5.cloned.1.call-update
  266.2 51.0 %attn_bwd.3 = (bf16[8,384,512]{2,1,0:T(8,128)(2,1)}, f32[8,256,512]{2,1,0:T(8,128)}, f32[8,512]{1,0:T(8,128)}) custom-call(s32[8]{0:T(128)} %len_ref.7, bf16[8,384,512]{2,1,0:T(8,128)(2,1)} %bitcast.22, bf16[8,384,512]{2,1,0:T(8,128)(2,1)} %x_ref.3, bf16[8,384,512]{2,1,0:T(8,128)(2,1)} %get-tuple-element.71.q_ref, ...), custom_call_target="tpu_custom_call" | custom-call | flops 30000001024 | bytes 50000000 | tf_op jit(solution)/shard_map/attn_bwd/pallas_call | solution.py:382
  317.3 29.3 %scatter_tail.1 = (f32[256,512]{1,0:T(8,128)}, f32[32,128]{1,0:T(8,128)}) custom-call(f32[8,256,512]{2,1,0:T(8,128)} %get-tuple-element.77.ga_ref, f32[8,512]{1,0:T(8,128)} %get-tuple-element.78.sa1_ref, f32[8,512]{1,0:T(8,128)} %get-tuple-element.79.sa0_ref, f32[8,512]{1,0:T(8,128)} %get-tuple-element.80.sm1_ref, f32[8,512]{1,0:T(8,128)} %get-tuple-element.81.sm0_ref), custom_call_target="tpu_custom_call" | custom-call | flops 1000000000 | bytes 8000000 | tf_op jit(solution)/shard_map/scatter_tail/pallas_call | solution.py:654
  346.6 0.0 reduce-scatter.3.cloned.1.call-done
  346.6 54.3 %reduce-scatter.5.cloned.1.call-done = f32[1,512,512]{2,1,0:T(8,128)} async-done(((f32[8,512,512]{2,1,0:T(8,128)}), f32[1,512,512]{2,1,0:T(8,128)}) %reduce-scatter.5.cloned.1.call-update) | async-done | bytes 1048592 | tf_op jit(solution)/shard_map/reduce_scatter | solution.py:723
  400.9 4.0 finish.1
Async XLA Ops:
  7.2 51.7 %all-gather.7.cloned.1.call-start = ((), (), s32[]{:S(2)}) async-start(), calls=%async_computation.4 | async-start | bytes 4718592 | tf_op jit(solution)/shard_map/all_gather | solution.py:695
  27.2 58.0 %all-gather.9.cloned.1.call-start = ((), (), s32[]{:S(2)}) async-start(), calls=%async_computation.5 | async-start | bytes 2359296 | tf_op jit(solution)/shard_map/all_gather | solution.py:695
  27.9 87.6 %all-gather.11.cloned.1.call-start = ((), (), s32[]{:S(2)}) async-start(), calls=%async_computation.6 | async-start | bytes 4718592 | tf_op jit(solution)/shard_map/all_gather | solution.py:695
  28.7 317.9 %reduce-scatter.3.cloned.1.call-start = ((), (), s32[]{:S(2)}) async-start(), calls=%async_computation.2 | async-start | bytes 9437184 | tf_op jit(solution)/shard_map/reduce_scatter | solution.py:723
  265.7 135.3 %reduce-scatter.5.cloned.1.call-start = ((), (), s32[]{:S(2)}) async-start(), calls=%async_computation.3 | async-start | bytes 9437184 | tf_op jit(solution)/shard_map/reduce_scatter | solution.py:723
Sparse Core Ops, SparseCore 0:
  27.3 31.0 all-gather.6
  60.2 22.2 all-gather.8
  84.3 30.9 all-gather.10
  265.8 67.7 reduce-scatter.2
  336.8 64.1 reduce-scatter.4
